TPU v7x, 256 devices: a whole 4x4x8 slice. The times are simulated.
256 devices in a mesh: terms: 256 (over z, y, x, core).
Axes of the slice: x: 4, y: 4, z: 8, core: 2. Of those that a mesh axis runs over, the one named last changes fastest.
Arguments:
- psi: float32 [256, 4, 4, 256], replicated
- left_env: bfloat16 [1536, 256, 256], P('terms')
- two_site: bfloat16 [1536, 16, 16], P('terms')
- right_env: bfloat16 [1536, 256, 256], P('terms')
Outputs:
- output 1: float32 [7, 256, 4, 4, 256], replicated
- output 2: float32 [6], replicated
- output 3: float32 [6], replicated
All inputs are finite; a program needn't handle non-finite values.
Results may differ from a plain program's by a relative error of at most 0.0153122.
Values are sent between devices in bfloat16 or wider.
A program may use at most 768 MiB of HBM per device.

v0:
```python
import jax
import jax.numpy as jnp
from jax import lax
from jax.sharding import PartitionSpec as P

LANCZOS_STEPS = 6


def solution(mesh):
    groups = mesh.shape["terms"]

    def local_sigma(vec_bf, left_loc, site_loc, right_loc):
        bond = vec_bf.shape[0]
        pair = site_loc.shape[1]
        vec_flat = vec_bf.reshape(bond * pair, bond)

        def one_term(acc_sum, term):
            left_k, site_k, right_k = term
            right_out = lax.dot_general(vec_flat, right_k, (((1,), (1,)), ((), ())), preferred_element_type=jnp.float32).astype(jnp.bfloat16)
            site_out = jnp.einsum("qp,xpb->xqb", site_k, right_out.reshape(bond, pair, bond), preferred_element_type=jnp.float32).astype(jnp.bfloat16)
            return acc_sum + jnp.dot(left_k, site_out.reshape(bond, pair * bond), preferred_element_type=jnp.float32), None

        init_acc = jnp.zeros((bond, pair * bond), jnp.float32)
        return lax.scan(one_term, init_acc, (left_loc, site_loc, right_loc))[0]

    def body(psi, left_loc, site_loc, right_loc):
        bond = psi.shape[0]
        slab = bond // groups
        row_start = lax.axis_index("terms") * slab
        cur_full = psi / jnp.sqrt(jnp.sum(psi * psi))
        cur_slab = lax.dynamic_slice_in_dim(cur_full, row_start, slab, axis=0)
        prev_slab = jnp.zeros_like(cur_slab)
        beta_prev = 0.0
        vectors = [cur_full]
        alphas = []
        betas = []
        for step_idx in range(LANCZOS_STEPS):
            part_sum = local_sigma(cur_full.astype(jnp.bfloat16), left_loc, site_loc, right_loc)
            sigma_slab = lax.psum_scatter(part_sum, "terms", scatter_dimension=0, tiled=True).reshape(cur_slab.shape)
            alpha = lax.psum(jnp.sum(sigma_slab * cur_slab), "terms")
            residual = sigma_slab - alpha * cur_slab - beta_prev * prev_slab
            beta = jnp.sqrt(lax.psum(jnp.sum(residual * residual), "terms"))
            prev_slab = cur_slab
            cur_slab = residual / beta
            cur_full = lax.all_gather(cur_slab, "terms", axis=0, tiled=True)
            vectors.append(cur_full)
            alphas.append(alpha)
            betas.append(beta)
            beta_prev = beta
        return jnp.stack(vectors), jnp.stack(alphas), jnp.stack(betas)

    return jax.shard_map(body, mesh=mesh, in_specs=(P(), P("terms"), P("terms"), P("terms")), out_specs=(P(), P(), P()), check_vma=False)
```

profile of v0, /device:TPU:1, one launch (start us, length us, event | category | flops | bytes accessed | tf_op | source)
XLA Modules:
  0.0 3759.7 jit_solution(12405372328063600961)
XLA Ops:
  7.2 5.0 multiply_reduce_fusion
  12.9 5.7 fusion.60
  20.7 79.4 %while.66 = (s32[]{:T(128)}, f32[256,4096]{1,0:T(8,128)}, bf16[6,256,256]{2,1,0:T(8,128)(2,1)S(1)}, bf16[6,256,256]{2,1,0:T(8,128)(2,1)}, bf16[4096,256]{1,0:T(8...) while((s32[]{:T(128)}, f32[256,4096]{1,0:T(8,128)}, ...), condition=%wide.region_2.3_spmd.clone, body=%wide.region_1.2_spmd.clone.sunk | while | flops 1111490560 | bytes 27529328 | solution.py:24
  40.7 4.9 convolution_add_fusion.12
  54.3 4.9 convolution_add_fusion.12
  67.9 4.9 convolution_add_fusion.12
  81.5 4.9 convolution_add_fusion.12
  95.2 4.9 convolution_add_fusion.12
  100.2 274.1 %all-reduce.13.cloned.1.call-done = f32[256,4096]{1,0:T(8,128)} async-done(((f32[256,4096]{1,0:T(8,128)}), f32[256,4096]{1,0:T(8,128)}) %all-reduce.13.cloned.1.call-update) | async-done | bytes 4194320
  376.6 77.6 %psum.84 = f32[]{:T(128)} all-reduce(f32[]{:T(128)} %multiply_reduce_fusion.12), channel_id=1, replica_groups=mesh['terms'=256] {'terms'}, use_global_device_ids=true, to_apply=%region_5.6 | all-reduce | flops 1 | bytes 8 | tf_op jit(solution)/shard_map/psum | solution.py:40
  456.2 73.3 %psum.85 = f32[]{:T(128)} all-reduce(f32[]{:T(128)} %multiply_reduce_fusion.11), channel_id=1, replica_groups=mesh['terms'=256] {'terms'}, use_global_device_ids=true, to_apply=%region_7.8 | all-reduce | flops 1 | bytes 8 | tf_op jit(solution)/shard_map/psum | solution.py:42
  532.7 112.6 %all-gather.7.cloned.1.call-done = f32[256,4,4,256]{3,2,1,0:T(4,128)} async-done(((f32[1,4,4,256]{3,2,1,0:T(4,128)}), f32[256,4,4,256]{3,2,1,0:T(4,128)}) %all-gather.7.cloned.1.call-update) | async-done | bytes 4194320 | tf_op jit(solution)/shard_map/all_gather | solution.py:45
  650.6 79.2 %while.67 = (s32[]{:T(128)}, f32[256,4096]{1,0:T(8,128)}, bf16[6,256,256]{2,1,0:T(8,128)(2,1)S(1)}, bf16[6,256,256]{2,1,0:T(8,128)(2,1)}, bf16[4096,256]{1,0:T(8...) while((s32[]{:T(128)}, f32[256,4096]{1,0:T(8,128)}, ...), condition=%wide.region_9.10_spmd.clone, body=%wide.region_8.9_spmd.clone.sunk | while | flops 1111490560 | bytes 27529328 | solution.py:24
  670.6 4.9 convolution_add_fusion.13
  684.2 4.9 convolution_add_fusion.13
  697.7 4.9 convolution_add_fusion.13
  711.3 4.9 convolution_add_fusion.13
  724.8 4.9 convolution_add_fusion.13
  729.9 267.4 %all-reduce.15.cloned.1.call-done = f32[256,4096]{1,0:T(8,128)} async-done(((f32[256,4096]{1,0:T(8,128)}), f32[256,4096]{1,0:T(8,128)}) %all-reduce.15.cloned.1.call-update) | async-done | bytes 4194320
  998.9 77.6 %psum.86 = f32[]{:T(128)} all-reduce(f32[]{:T(128)} %multiply_reduce_fusion.10), channel_id=1, replica_groups=mesh['terms'=256] {'terms'}, use_global_device_ids=true, to_apply=%region_12.13 | all-reduce | flops 1 | bytes 8 | tf_op jit(solution)/shard_map/psum | solution.py:40
  1078.4 73.3 %psum.87 = f32[]{:T(128)} all-reduce(f32[]{:T(128)} %get-tuple-element.407), channel_id=1, replica_groups=mesh['terms'=256] {'terms'}, use_global_device_ids=true, to_apply=%region_14.15 | all-reduce | flops 1 | bytes 8 | tf_op jit(solution)/shard_map/psum | solution.py:42
  1153.1 113.1 %all-gather.9.cloned.1.call-done = f32[256,4,4,256]{3,2,1,0:T(4,128)} async-done(((f32[1,4,4,256]{3,2,1,0:T(4,128)}), f32[256,4,4,256]{3,2,1,0:T(4,128)}) %all-gather.9.cloned.1.call-update) | async-done | bytes 4194320 | tf_op jit(solution)/shard_map/all_gather | solution.py:45
  1271.5 79.4 %while.68 = (s32[]{:T(128)}, f32[256,4096]{1,0:T(8,128)}, bf16[6,256,256]{2,1,0:T(8,128)(2,1)S(1)}, bf16[6,256,256]{2,1,0:T(8,128)(2,1)}, bf16[4096,256]{1,0:T(8...) while((s32[]{:T(128)}, f32[256,4096]{1,0:T(8,128)}, ...), condition=%wide.region_16.17_spmd.clone, body=%wide.region_15.16_spmd.clone.sunk | while | flops 1111490560 | bytes 27529328 | solution.py:24
  1291.5 4.9 convolution_add_fusion.14
  1305.1 4.9 convolution_add_fusion.14
  1318.7 4.9 convolution_add_fusion.14
  1332.3 4.9 convolution_add_fusion.14
  1345.9 4.9 convolution_add_fusion.14
  1350.9 267.4 %all-reduce.17.cloned.1.call-done = f32[256,4096]{1,0:T(8,128)} async-done(((f32[256,4096]{1,0:T(8,128)}), f32[256,4096]{1,0:T(8,128)}) %all-reduce.17.cloned.1.call-update) | async-done | bytes 4194320
  1619.9 77.8 %psum.88 = f32[]{:T(128)} all-reduce(f32[]{:T(128)} %multiply_reduce_fusion.8), channel_id=1, replica_groups=mesh['terms'=256] {'terms'}, use_global_device_ids=true, to_apply=%region_19.20 | all-reduce | flops 1 | bytes 8 | tf_op jit(solution)/shard_map/psum | solution.py:40
  1698.9 73.3 %psum.89 = f32[]{:T(128)} all-reduce(f32[]{:T(128)} %get-tuple-element.405), channel_id=1, replica_groups=mesh['terms'=256] {'terms'}, use_global_device_ids=true, to_apply=%region_21.22 | all-reduce | flops 1 | bytes 8 | tf_op jit(solution)/shard_map/psum | solution.py:42
  1773.5 113.1 %all-gather.11.cloned.1.call-done = f32[256,4,4,256]{3,2,1,0:T(4,128)} async-done(((f32[1,4,4,256]{3,2,1,0:T(4,128)}), f32[256,4,4,256]{3,2,1,0:T(4,128)}) %all-gather.11.cloned.1.call-update) | async-done | bytes 4194320 | tf_op jit(solution)/shard_map/all_gather | solution.py:45
  1891.9 79.2 %while.69 = (s32[]{:T(128)}, f32[256,4096]{1,0:T(8,128)}, bf16[6,256,256]{2,1,0:T(8,128)(2,1)S(1)}, bf16[6,256,256]{2,1,0:T(8,128)(2,1)}, bf16[4096,256]{1,0:T(8...) while((s32[]{:T(128)}, f32[256,4096]{1,0:T(8,128)}, ...), condition=%wide.region_23.24_spmd.clone, body=%wide.region_22.23_spmd.clone.sunk | while | flops 1111490560 | bytes 27529328 | solution.py:24
  1911.9 4.9 convolution_add_fusion.15
  1925.4 4.9 convolution_add_fusion.15
  1939.0 4.9 convolution_add_fusion.15
  1952.5 4.9 convolution_add_fusion.15
  1966.1 4.9 convolution_add_fusion.15
  1971.1 267.4 %all-reduce.19.cloned.1.call-done = f32[256,4096]{1,0:T(8,128)} async-done(((f32[256,4096]{1,0:T(8,128)}), f32[256,4096]{1,0:T(8,128)}) %all-reduce.19.cloned.1.call-update) | async-done | bytes 4194320
  2240.1 77.6 %psum.90 = f32[]{:T(128)} all-reduce(f32[]{:T(128)} %multiply_reduce_fusion.6), channel_id=1, replica_groups=mesh['terms'=256] {'terms'}, use_global_device_ids=true, to_apply=%region_26.27 | all-reduce | flops 1 | bytes 8 | tf_op jit(solution)/shard_map/psum | solution.py:40
  2318.8 73.3 %psum.91 = f32[]{:T(128)} all-reduce(f32[]{:T(128)} %get-tuple-element.403), channel_id=1, replica_groups=mesh['terms'=256] {'terms'}, use_global_device_ids=true, to_apply=%region_28.29 | all-reduce | flops 1 | bytes 8 | tf_op jit(solution)/shard_map/psum | solution.py:42
  2393.7 112.8 %all-gather.13.cloned.1.call-done = f32[256,4,4,256]{3,2,1,0:T(4,128)} async-done(((f32[1,4,4,256]{3,2,1,0:T(4,128)}), f32[256,4,4,256]{3,2,1,0:T(4,128)}) %all-gather.13.cloned.1.call-update) | async-done | bytes 4194320 | tf_op jit(solution)/shard_map/all_gather | solution.py:45
  2511.8 79.4 %while.70 = (s32[]{:T(128)}, f32[256,4096]{1,0:T(8,128)}, bf16[6,256,256]{2,1,0:T(8,128)(2,1)S(1)}, bf16[6,256,256]{2,1,0:T(8,128)(2,1)}, bf16[4096,256]{1,0:T(8...) while((s32[]{:T(128)}, f32[256,4096]{1,0:T(8,128)}, ...), condition=%wide.region_30.31_spmd.clone, body=%wide.region_29.30_spmd.clone.sunk | while | flops 1111490560 | bytes 27529328 | solution.py:24
  2531.9 4.9 convolution_add_fusion.16
  2545.5 4.9 convolution_add_fusion.16
  2559.1 4.9 convolution_add_fusion.16
  2572.7 4.9 convolution_add_fusion.16
  2586.3 4.9 convolution_add_fusion.16
  2591.3 267.4 %all-reduce.21.cloned.1.call-done = f32[256,4096]{1,0:T(8,128)} async-done(((f32[256,4096]{1,0:T(8,128)}), f32[256,4096]{1,0:T(8,128)}) %all-reduce.21.cloned.1.call-update) | async-done | bytes 4194320
  2860.3 77.6 %psum.92 = f32[]{:T(128)} all-reduce(f32[]{:T(128)} %multiply_reduce_fusion.4), channel_id=1, replica_groups=mesh['terms'=256] {'terms'}, use_global_device_ids=true, to_apply=%region_33.34 | all-reduce | flops 1 | bytes 8 | tf_op jit(solution)/shard_map/psum | solution.py:40
  2939.1 73.3 %psum.93 = f32[]{:T(128)} all-reduce(f32[]{:T(128)} %get-tuple-element.401), channel_id=1, replica_groups=mesh['terms'=256] {'terms'}, use_global_device_ids=true, to_apply=%region_35.36 | all-reduce | flops 1 | bytes 8 | tf_op jit(solution)/shard_map/psum | solution.py:42
  3013.8 113.1 %all-gather.15.cloned.1.call-done = f32[256,4,4,256]{3,2,1,0:T(4,128)} async-done(((f32[1,4,4,256]{3,2,1,0:T(4,128)}), f32[256,4,4,256]{3,2,1,0:T(4,128)}) %all-gather.15.cloned.1.call-update) | async-done | bytes 4194320 | tf_op jit(solution)/shard_map/all_gather | solution.py:45
  3132.2 79.2 %while.71 = (s32[]{:T(128)}, f32[256,4096]{1,0:T(8,128)}, bf16[6,256,256]{2,1,0:T(8,128)(2,1)S(1)}, bf16[6,256,256]{2,1,0:T(8,128)(2,1)}, bf16[4096,256]{1,0:T(8...) while((s32[]{:T(128)}, f32[256,4096]{1,0:T(8,128)}, ...), condition=%wide.region_37.38_spmd.clone, body=%wide.region_36.37_spmd.clone.sunk | while | flops 1111490560 | bytes 27529328 | solution.py:24
  3152.2 4.9 convolution_add_fusion.17
  3165.7 4.9 convolution_add_fusion.17
  3179.3 4.9 convolution_add_fusion.17
  3192.8 4.9 convolution_add_fusion.17
  3206.4 4.9 convolution_add_fusion.17
  3211.4 267.4 %all-reduce.23.cloned.1.call-done = f32[256,4096]{1,0:T(8,128)} async-done(((f32[256,4096]{1,0:T(8,128)}), f32[256,4096]{1,0:T(8,128)}) %all-reduce.23.cloned.1.call-update) | async-done | bytes 4194320
  3480.4 77.8 %psum.94 = f32[]{:T(128)} all-reduce(f32[]{:T(128)} %multiply_reduce_fusion.2), channel_id=1, replica_groups=mesh['terms'=256] {'terms'}, use_global_device_ids=true, to_apply=%region_40.41 | all-reduce | flops 1 | bytes 8 | tf_op jit(solution)/shard_map/psum | solution.py:40
  3559.5 73.3 %psum.95 = f32[]{:T(128)} all-reduce(f32[]{:T(128)} %get-tuple-element.399), channel_id=1, replica_groups=mesh['terms'=256] {'terms'}, use_global_device_ids=true, to_apply=%region_42.43 | all-reduce | flops 1 | bytes 8 | tf_op jit(solution)/shard_map/psum | solution.py:42
  3634.1 5.3 bitcast_dynamic-update-slice_fusion.6
  3659.4 87.9 %all-gather.17.cloned.1.call-done = f32[256,4,4,256]{3,2,1,0:T(4,128)} async-done(((f32[1,4,4,256]{3,2,1,0:T(4,128)}), f32[256,4,4,256]{3,2,1,0:T(4,128)}) %all-gather.17.cloned.1.call-update) | async-done | bytes 4194320 | tf_op jit(solution)/shard_map/all_gather | solution.py:45
  3747.2 5.2 bitcast_dynamic-update-slice_fusion
  (244 shorter events, 400.4 us)
Async XLA Ops:
  7.2 367.2 %all-reduce.13.cloned.1.call-start = ((), (), s32[]{:S(2)}) async-start(), calls=%async_computation.6 | async-start | bytes 8388608
  18.6 2.1 copy-start
  18.6 2.1 copy-start.6
  100.1 545.2 %all-gather.7.cloned.1.call-start = ((), (), s32[]{:S(2)}) async-start(), calls=%async_computation | async-start | bytes 4210688 | tf_op jit(solution)/shard_map/all_gather | solution.py:45
  532.2 465.1 %all-reduce.15.cloned.1.call-start = ((), (), s32[]{:S(2)}) async-start(), calls=%async_computation.7 | async-start | bytes 8388608
  729.8 268.5 %copy-start.7 = (f32[1,4,4,256]{3,2,1,0:T(4,128)S(1)}, f32[1,4,4,256]{3,2,1,0:T(4,128)}, u32[]{:S(2)}) copy-start(f32[1,4,4,256]{3,2,1,0:T(4,128)} %broadcast_divide_fusion.6) | copy-start | bytes 49156
  729.8 536.3 %all-gather.9.cloned.1.call-start = ((), (), s32[]{:S(2)}) async-start(), calls=%async_computation.1 | async-start | bytes 4210688 | tf_op jit(solution)/shard_map/all_gather | solution.py:45
  1153.0 465.2 %all-reduce.17.cloned.1.call-start = ((), (), s32[]{:S(2)}) async-start(), calls=%async_computation.8 | async-start | bytes 8388608
  1350.9 535.7 %all-gather.11.cloned.1.call-start = ((), (), s32[]{:S(2)}) async-start(), calls=%async_computation.2 | async-start | bytes 4210688 | tf_op jit(solution)/shard_map/all_gather | solution.py:45
  1773.5 465.0 %all-reduce.19.cloned.1.call-start = ((), (), s32[]{:S(2)}) async-start(), calls=%async_computation.9 | async-start | bytes 8388608
  1971.1 535.5 %all-gather.13.cloned.1.call-start = ((), (), s32[]{:S(2)}) async-start(), calls=%async_computation.3 | async-start | bytes 4210688 | tf_op jit(solution)/shard_map/all_gather | solution.py:45
  2393.4 465.3 %all-reduce.21.cloned.1.call-start = ((), (), s32[]{:S(2)}) async-start(), calls=%async_computation.10 | async-start | bytes 8388608
  2591.3 535.6 %all-gather.15.cloned.1.call-start = ((), (), s32[]{:S(2)}) async-start(), calls=%async_computation.4 | async-start | bytes 4210688 | tf_op jit(solution)/shard_map/all_gather | solution.py:45
  3013.7 465.1 %all-reduce.23.cloned.1.call-start = ((), (), s32[]{:S(2)}) async-start(), calls=%async_computation.11 | async-start | bytes 8388608
  3211.4 535.9 %all-gather.17.cloned.1.call-start = ((), (), s32[]{:S(2)}) async-start(), calls=%async_computation.5 | async-start | bytes 4210688 | tf_op jit(solution)/shard_map/all_gather | solution.py:45
  3634.1 5.4 copy-start.1
  3639.5 3.0 copy-start.2
  3642.5 3.0 copy-start.3
  3645.5 3.0 copy-start.4
  3648.5 3.0 copy-start.5
Sparse Core Ops, SparseCore 0:
  100.2 274.0 all-reduce.12
  532.3 112.9 all-gather.6
  729.9 267.2 all-reduce.14
  1153.1 112.9 all-gather.8
  1351.0 267.2 all-reduce.16
  1773.6 112.9 all-gather.10
  1971.2 267.2 all-reduce.18
  2393.6 112.9 all-gather.12
  2591.4 267.2 all-reduce.20
  3013.9 112.9 all-gather.14
  3211.5 267.2 all-reduce.22
  3634.2 112.9 all-gather.16
where the time goes:
time: 3770 us; the launch traced here: 3760 us
  waiting for transfers between devices  2260 us (60%)
  blocking collectives  906 us (24%)
  matrix products  324 us (9%)
  local copies, waits for them, and re-layouts  200 us (5%)
  other arithmetic  44.9 us (1%)
    unnamed x18, waiting for transfers between devices  1610 us
    all_gather x6, waiting for transfers between devices, body(): cur_full = lax.all_gather(cur_slab, 'terms', axis=0, tiled=True)  652 us
    psum x6, blocking collectives, body(): alpha = lax.psum(jnp.sum(sigma_slab * cur_slab), 'terms')  466 us
    psum x6, blocking collectives, body(): beta = jnp.sqrt(lax.psum(jnp.sum(residual * residual), 'terms'))  440 us
    dot_general x36, matrix products, one_term(): jnp.dot(left_k, site_out.reshape(bond, pair * bond), preferred_element_ty...  165 us
    dot_general x36, matrix products, one_term(): lax.dot_general(vec_flat, right_k, (((1,), (1,)), ((), ())), preferred_el...  134 us
    convert_element_type x36, local copies, waits for them, and re-layouts, one_term(): lax.dot_general(vec_flat, right_k, (((1,), (1,)), ((), ())), preferred_el...  118 us
  transfers between devices with their start and end apart: 12, of which 12 were waited for; matrix products, arithmetic and copies ran while one was open for 1% of the time, Pallas kernels for 0%

commit v1 on v0

v1 whole, which is shorter than its diff:
```python
import jax
import jax.numpy as jnp
from jax import lax
from jax.experimental import pallas as pl
from jax.experimental.pallas import tpu as pltpu
from jax.sharding import PartitionSpec as P

STEPS = 6
D = 256
PAIR = 16
ROWS = PAIR * D
LANES = 128
TERMS = 6
XN, YN, ZN = 4, 4, 8
F32 = jnp.float32
BF16 = jnp.bfloat16
MESH_ID = pl.DeviceIdType.MESH

S1, S2, S3, S4, S5, S6 = range(6)
T1, T2, T3, T4, T5, T6 = range(6, 12)
ZR = 12
ZG = 19
G1, G2, G3, G4 = range(26, 30)
H1, H2, H3, H4 = range(30, 34)
NSEM = 34
CROSS = 5


def rows(start, size):
    return pl.ds(pl.multiple_of(start, 8), size)


def lanczos(psi_hbm, left_hbm, kron_hbm, right_hbm, kry, ab, u, y1a, y1b, y2, part, lbuf, rbuf, wbuf, relay1, final1, relay2, final2, zrecv, load_sem, send_sem, recv_sem, c_send, c_recv, x_send, x_recv):
    me = lax.axis_index("terms")
    core = me % 2
    x = (me // 2) % XN
    y = (me // 8) % YN
    z = me // 32

    def dev(xx, yy, zz, cc):
        return (((zz * YN + yy) * XN + xx) * 2 + cc,)

    xr, xl = dev((x + 1) % XN, y, z, core), dev((x + 3) % XN, y, z, core)
    yr, yl = dev(x, (y + 1) % YN, z, core), dev(x, (y + 3) % YN, z, core)
    zdev = [None] + [dev(x, y, (z + d) % ZN, core) for d in range(1, ZN)]
    other = dev(x, y, z, 1 - core)

    barrier = pltpu.get_barrier_semaphore()
    peers = [xr, xl, yr, yl, other] + zdev[1:]
    for peer in peers:
        pl.semaphore_signal(barrier, inc=1, device_id=peer, device_id_type=MESH_ID)

    loads = []
    for h in range(2):
        for s in range(4):
            for t in range(4):
                loads.append(pltpu.make_async_copy(psi_hbm.at[:, s, t, pl.ds(h * LANES, LANES)], kry.at[0, h, pl.ds((s * 4 + t) * D, D)], load_sem.at[0]))
    for cp in loads:
        cp.start()
    mine = pl.multiple_of(core * TERMS, TERMS)
    own = []
    for k in range(TERMS):
        own.append(pltpu.make_async_copy(left_hbm.at[k], lbuf.at[:, pl.ds(pl.multiple_of((mine + k) * D, D), D)], load_sem.at[1]))
        own.append(pltpu.make_async_copy(right_hbm.at[k, :, pl.ds(pl.multiple_of(core * LANES, LANES), LANES)], rbuf.at[mine + k], load_sem.at[1]))
    own.append(pltpu.make_async_copy(kron_hbm, wbuf.at[pl.ds(mine, TERMS)], load_sem.at[1]))
    for cp in own:
        cp.start()

    pl.semaphore_wait(barrier, len(peers))

    swaps = []
    for k in range(TERMS):
        swaps.append(pltpu.make_async_remote_copy(left_hbm.at[k], lbuf.at[:, pl.ds(pl.multiple_of((mine + k) * D, D), D)], x_send.at[2 * k], x_recv.at[2 * k], device_id=other, device_id_type=MESH_ID))
        swaps.append(pltpu.make_async_remote_copy(right_hbm.at[k, :, pl.ds(pl.multiple_of((1 - core) * LANES, LANES), LANES)], rbuf.at[mine + k], x_send.at[2 * k + 1], x_recv.at[2 * k + 1], device_id=other, device_id_type=MESH_ID))
    swaps.append(pltpu.make_async_remote_copy(kron_hbm, wbuf.at[pl.ds(mine, TERMS)], x_send.at[2 * TERMS], x_recv.at[2 * TERMS], device_id=other, device_id_type=MESH_ID))
    for cp in swaps:
        cp.start()

    CH = 64
    NCH = ROWS // CH

    for cp in loads:
        cp.wait()

    def chunk(i):
        return i // NCH, rows((i % NCH) * CH, CH)

    def sumsq(i, acc):
        h, r = chunk(i)
        val = kry[0, h, r, :]
        return acc + val * val

    zero = jnp.zeros((CH, LANES), F32)

    def total(acc):
        return jnp.broadcast_to(jnp.sum(acc, keepdims=True), (8, LANES))

    norm0 = jnp.sqrt(total(lax.fori_loop(0, 2 * NCH, sumsq, zero)))
    inv0 = jnp.broadcast_to((1.0 / norm0)[:1], (CH, LANES))

    def scale0(i, carry):
        h, r = chunk(i)
        val = kry[0, h, r, :] * inv0
        kry[0, h, r, :] = val
        u[h, r, :] = val.astype(BF16)
        return carry

    lax.fori_loop(0, 2 * NCH, scale0, 0)
    for cp in own:
        cp.wait()
    for cp in swaps:
        cp.wait()

    def right_product(g, out):
        weights = jnp.concatenate([rbuf[2 * g], rbuf[2 * g + 1]], axis=1)
        for m in range(4):
            r = pl.ds(m * 1024, 1024)
            lhs = jnp.concatenate([u[0, r, :], u[1, r, :]], axis=1)
            res = jnp.dot(lhs, weights, preferred_element_type=F32).astype(BF16)
            out[0, r, :] = res[:, :LANES]
            out[1, r, :] = res[:, LANES:]

    def site_product(g, src):
        for t in range(2):
            k = 2 * g + t
            w = wbuf[k]
            for m in range(8):
                cols = []
                for b in range(2):
                    cols.append(jnp.concatenate([src[t, pl.ds(p * D + 32 * m + 16 * b, 16), :] for p in range(PAIR)], axis=0))
                res = jnp.dot(w, jnp.concatenate(cols, axis=1), preferred_element_type=F32).astype(BF16)
                for b in range(2):
                    for q in range(PAIR):
                        y2[q, rows(k * D + 32 * m + 16 * b, 16), :] = res[16 * q : 16 * q + 16, b * LANES : (b + 1) * LANES]

    def left_product(qa, qb):
        rhs = jnp.concatenate([y2[qa], y2[qa + 1], y2[qb], y2[qb + 1]], axis=1)
        res = jnp.dot(lbuf[...], rhs, preferred_element_type=F32)
        for i, q in enumerate((qa, qa + 1, qb, qb + 1)):
            part[rows(q * D, D), :] = res[:, i * LANES : (i + 1) * LANES]

    def step(j, beta_prev):
        nxt = j + 1

        def remote(src, dst, p, s, device):
            return pltpu.make_async_remote_copy(src, dst, send_sem.at[p, s], recv_sem.at[p, s], device_id=device, device_id_type=MESH_ID)

        right_product(0, y1a)

        def two_pairs(i, carry):
            right_product(2 * i + 1, y1b)
            site_product(2 * i, y1a)
            right_product(2 * i + 2, y1a)
            site_product(2 * i + 1, y1b)
            return carry

        lax.fori_loop(0, 2, two_pairs, 0)
        right_product(5, y1b)
        site_product(4, y1a)
        site_product(5, y1b)

        ring1 = [(x, xr, xl, 0), (y, yr, yl, ROWS // 2)]
        ring2 = [(y, yr, yl, 512 * x), (x, xr, xl, ROWS // 2 + 512 * y)]
        sends = []

        def start(cp):
            cp.start()
            sends.append(cp)
            return cp

        def at1(p, d, off, size):
            pos, _, _, base = ring1[p]
            return rows(base + 512 * ((pos + d) % 4) + off, size)

        def at2(p, d, off, size):
            pos, _, _, base = ring2[p]
            return rows(base + 128 * ((pos + d) % 4) + off, size)

        waits = [[None] * 6 for _ in range(2)]
        for d in (2, 1, 3, 0):
            left_product(2 * ((x + d) % 4), 8 + 2 * ((y + d) % 4))
            for p in range(2):
                _, right, left, _ = ring1[p]
                if d == 2:
                    waits[p][0] = start(remote(part.at[at1(p, 2, 0, 256)], relay1.at[p, 0], p, S1, right))
                    waits[p][1] = start(remote(part.at[at1(p, 2, 256, 256)], relay1.at[p, 1], p, S2, left))
                elif d == 1:
                    waits[p][2] = start(remote(part.at[at1(p, 1, 256, 256)], final1.at[p, 0, pl.ds(256, 256)], p, S3, right))
                elif d == 3:
                    waits[p][3] = start(remote(part.at[at1(p, 3, 0, 256)], final1.at[p, 1, pl.ds(0, 256)], p, S4, left))

        def add_into(dst_rows, size, refs):
            for o in range(0, size, 128):
                n = min(128, size - o)
                r = pl.ds(pl.multiple_of(dst_rows.start + o, 8), n)
                acc = part[r, :]
                for ref in refs:
                    acc = acc + ref[pl.ds(o, n), :]
                part[r, :] = acc

        for p in range(2):
            _, right, left, _ = ring1[p]
            waits[p][0].wait_recv()
            add_into(at1(p, 1, 0, 256), 256, [relay1.at[p, 0]])
            waits[p][4] = start(remote(part.at[at1(p, 1, 0, 256)], final1.at[p, 0, pl.ds(0, 256)], p, S5, right))
            waits[p][1].wait_recv()
            add_into(at1(p, 3, 256, 256), 256, [relay1.at[p, 1]])
            waits[p][5] = start(remote(part.at[at1(p, 3, 256, 256)], final1.at[p, 1, pl.ds(256, 256)], p, S6, left))
        for p in range(2):
            for i in (2, 3, 4, 5):
                waits[p][i].wait_recv()
            add_into(at1(p, 0, 0, 512), 512, [final1.at[p, 0], final1.at[p, 1]])

        for p in range(2):
            _, right, left, _ = ring2[p]
            waits[p][0] = start(remote(part.at[at2(p, 2, 0, 64)], relay2.at[p, 0], p, T1, right))
            waits[p][1] = start(remote(part.at[at2(p, 2, 64, 64)], relay2.at[p, 1], p, T2, left))
            waits[p][2] = start(remote(part.at[at2(p, 1, 64, 64)], final2.at[p, 0, pl.ds(64, 64)], p, T3, right))
            waits[p][3] = start(remote(part.at[at2(p, 3, 0, 64)], final2.at[p, 1, pl.ds(0, 64)], p, T4, left))
        for p in range(2):
            _, right, left, _ = ring2[p]
            waits[p][0].wait_recv()
            add_into(at2(p, 1, 0, 64), 64, [relay2.at[p, 0]])
            waits[p][4] = start(remote(part.at[at2(p, 1, 0, 64)], final2.at[p, 0, pl.ds(0, 64)], p, T5, right))
            waits[p][1].wait_recv()
            add_into(at2(p, 3, 64, 64), 64, [relay2.at[p, 1]])
            waits[p][5] = start(remote(part.at[at2(p, 3, 64, 64)], final2.at[p, 1, pl.ds(64, 64)], p, T6, left))
        for p in range(2):
            for i in (2, 3, 4, 5):
                waits[p][i].wait_recv()
            add_into(at2(p, 0, 0, 128), 128, [final2.at[p, 0], final2.at[p, 1]])

        mid = [512 * x + 128 * y, ROWS // 2 + 512 * y + 128 * x]
        zcopies = []
        for d in (4, 3, 5, 2, 6, 1, 7):
            for p in range(2):
                zcopies.append(start(remote(part.at[rows(mid[p] + 16 * ((z + d) % ZN), 16)], zrecv.at[p, d], p, ZR + d - 1, zdev[d])))
        for cp in zcopies:
            cp.wait_recv()
        own_rows = [rows(mid[p] + 16 * z, 16) for p in range(2)]
        for p in range(2):
            acc = part[own_rows[p], :]
            for d in range(1, ZN):
                acc = acc + zrecv[p, d]
            kry[nxt, core, own_rows[p], :] = acc

        zcopies = []
        for d in (4, 3, 5, 2, 6, 1, 7):
            for p in range(2):
                zcopies.append(start(remote(kry.at[nxt, core, own_rows[p]], kry.at[nxt, core, own_rows[p]], p, ZG + d - 1, zdev[d])))
        for cp in zcopies:
            cp.wait_recv()

        def spread(p, src_rows, s, device):
            return start(remote(kry.at[nxt, core, src_rows], kry.at[nxt, core, src_rows], p, s, device))

        g = [[None] * 4 for _ in range(2)]
        for p in range(2):
            _, right, left, _ = ring2[p]
            g[p][0] = spread(p, at2(p, 0, 0, 128), G1, right)
            g[p][1] = spread(p, at2(p, 0, 0, 128), G2, left)
        for p in range(2):
            _, right, left, _ = ring2[p]
            g[p][0].wait_recv()
            g[p][2] = spread(p, at2(p, 3, 0, 64), G3, right)
            g[p][1].wait_recv()
            g[p][3] = spread(p, at2(p, 1, 64, 64), G4, left)
        for p in range(2):
            g[p][2].wait_recv()
            g[p][3].wait_recv()
        h = [[None] * 4 for _ in range(2)]
        crossing = []
        turn = j % 2

        def cross(p, src_rows, i):
            cp = pltpu.make_async_remote_copy(kry.at[nxt, core, src_rows], kry.at[nxt, core, src_rows], c_send.at[turn, p, i], c_recv.at[turn, p, i], device_id=other, device_id_type=MESH_ID)
            crossing.append(start(cp))

        for p in range(2):
            _, right, left, _ = ring1[p]
            h[p][0] = spread(p, at1(p, 0, 0, 512), H1, right)
            h[p][1] = spread(p, at1(p, 0, 0, 512), H2, left)
            cross(p, at1(p, 0, 0, 512), 0)
        for p in range(2):
            _, right, left, _ = ring1[p]
            h[p][0].wait_recv()
            h[p][2] = spread(p, at1(p, 3, 0, 256), H3, right)
            cross(p, at1(p, 3, 0, 512), 1)
            h[p][1].wait_recv()
            h[p][3] = spread(p, at1(p, 1, 256, 256), H4, left)
            cross(p, at1(p, 1, 0, 512), 2)
        for p in range(2):
            h[p][2].wait_recv()
            cross(p, at1(p, 2, 0, 256), 3)
            h[p][3].wait_recv()
            cross(p, at1(p, 2, 256, 256), 4)
        for cp in crossing:
            cp.wait_recv()
        for cp in sends:
            cp.wait_send()

        prev = jnp.maximum(j - 1, 0)

        def dot_chunk(i, acc):
            hh, r = chunk(i)
            return acc + kry[nxt, hh, r, :] * kry[j, hh, r, :]

        alpha = total(lax.fori_loop(0, 2 * NCH, dot_chunk, zero))
        al = jnp.broadcast_to(alpha[:1], (CH, LANES))
        bp = jnp.broadcast_to(beta_prev[:1], (CH, LANES))

        def resid_chunk(i, acc):
            hh, r = chunk(i)
            val = kry[nxt, hh, r, :] - al * kry[j, hh, r, :] - bp * kry[prev, hh, r, :]
            kry[nxt, hh, r, :] = val
            return acc + val * val

        beta = jnp.sqrt(total(lax.fori_loop(0, 2 * NCH, resid_chunk, zero)))
        inv = jnp.broadcast_to((1.0 / beta)[:1], (CH, LANES))

        def scale_chunk(i, carry):
            hh, r = chunk(i)
            val = kry[nxt, hh, r, :] * inv
            kry[nxt, hh, r, :] = val
            u[hh, r, :] = val.astype(BF16)
            return carry

        lax.fori_loop(0, 2 * NCH, scale_chunk, 0)
        ab[0, j] = alpha
        ab[1, j] = beta
        return beta

    lax.fori_loop(0, STEPS, step, jnp.zeros((8, LANES), F32))


def write_out(kry, out, sem):
    copies = []
    for h in range(2):
        for s in range(4):
            for t in range(4):
                copies.append(pltpu.make_async_copy(kry.at[:, h, pl.ds((s * 4 + t) * D, D)], out.at[:, :, s, t, pl.ds(h * LANES, LANES)], sem))
    for cp in copies:
        cp.start()
    for cp in copies:
        cp.wait()


def solution(mesh):
    anywhere = pl.BlockSpec(memory_space=pl.ANY)
    vmem = pl.BlockSpec(memory_space=pltpu.VMEM)

    def body(psi, left_loc, site_loc, right_loc):
        eye = jnp.eye(16, dtype=BF16)
        kron = (site_loc[:, :, None, :, None] * eye[None, None, :, None, :]).reshape(TERMS, D, D)
        kry, ab = pl.pallas_call(
            lanczos,
            out_shape=(pltpu.VMEM((STEPS + 1, 2, ROWS, LANES), F32), pltpu.VMEM((2, STEPS, 8, LANES), F32)),
            in_specs=[anywhere] * 4,
            out_specs=(vmem, vmem),
            scratch_shapes=[
                pltpu.VMEM((2, ROWS, LANES), BF16),
                pltpu.VMEM((2, ROWS, LANES), BF16),
                pltpu.VMEM((2, ROWS, LANES), BF16),
                pltpu.VMEM((PAIR, 2 * TERMS * D, LANES), BF16),
                pltpu.VMEM((ROWS, LANES), F32),
                pltpu.VMEM((D, 2 * TERMS * D), BF16),
                pltpu.VMEM((2 * TERMS, D, LANES), BF16),
                pltpu.VMEM((2 * TERMS, D, D), BF16),
                pltpu.VMEM((2, 2, 256, LANES), F32),
                pltpu.VMEM((2, 2, 512, LANES), F32),
                pltpu.VMEM((2, 2, 64, LANES), F32),
                pltpu.VMEM((2, 2, 128, LANES), F32),
                pltpu.VMEM((2, ZN, 16, LANES), F32),
                pltpu.SemaphoreType.DMA((2,)),
                pltpu.SemaphoreType.DMA((2, NSEM)),
                pltpu.SemaphoreType.DMA((2, NSEM)),
                pltpu.SemaphoreType.DMA((2, 2, CROSS)),
                pltpu.SemaphoreType.DMA((2, 2, CROSS)),
                pltpu.SemaphoreType.DMA((2 * TERMS + 1,)),
                pltpu.SemaphoreType.DMA((2 * TERMS + 1,)),
            ],
            compiler_params=pltpu.CompilerParams(collective_id=0, has_side_effects=True, vmem_limit_bytes=30 * 2**20),
            name="lanczos",
        )(*(pltpu.with_memory_space_constraint(arr, pltpu.HBM) for arr in (psi, left_loc, kron, right_loc)))
        krylov = pl.pallas_call(
            write_out,
            out_shape=jax.ShapeDtypeStruct((STEPS + 1, D, 4, 4, D), F32),
            in_specs=[vmem],
            out_specs=anywhere,
            scratch_shapes=[pltpu.SemaphoreType.DMA],
            compiler_params=pltpu.CompilerParams(vmem_limit_bytes=2**20),
            name="write_out",
        )(pltpu.with_memory_space_constraint(kry, pltpu.VMEM))
        return krylov, ab[0, :, 0, 0], ab[1, :, 0, 0]

    return jax.shard_map(body, mesh=mesh, in_specs=(P(), P("terms"), P("terms"), P("terms")), out_specs=(P(), P(), P()), check_vma=False)
```

time: 3770 us -> 436 us (0.12)
  waiting for transfers between devices: 2260 us -> 0 us
  blocking collectives: 906 us -> 0 us
  Pallas kernels: 0 us -> 420 us
  matrix products: 324 us -> 0 us
  local copies, waits for them, and re-layouts: 200 us -> 13.9 us
  other arithmetic: 44.9 us -> 0.95 us
    unnamed x18 -> x0, waiting for transfers between devices: 1610 us -> none
    psum x12 -> x0, blocking collectives: 906 us -> none  [the longest x6 466 us: body(): alpha = lax.psum(jnp.sum(sigma_slab * cur_slab), 'terms')]
    all_gather x6 -> x0, waiting for transfers between devices: 652 us -> none  [body(): cur_full = lax.all_gather(cur_slab, 'terms', axis=0, tiled=True)]
    pallas_call x0 -> x2, Pallas kernels: none -> 420 us  [the longest x1 411 us: body(): pl.pallas_call(lanczos, out_shape=(pltpu.VMEM((STEPS + 1, 2, ROWS, LANES)...]
    dot_general x108 -> x0, matrix products: 324 us -> none  [the longest x36 165 us: one_term(): jnp.dot(left_k, site_out.reshape(bond, pair * bond), preferred_element_ty...]
    convert_element_type x36 -> x0, local copies, waits for them, and re-layouts: 118 us -> none  [one_term(): lax.dot_general(vec_flat, right_k, (((1,), (1,)), ((), ())), preferred_el...]
  transfers between devices with their start and end apart: 12 -> 0, of which waited for: 12 -> 0; matrix products, arithmetic and copies ran while one was open for 1% -> 0% of each run, Pallas kernels for 0% -> 0%
where the time goes in v1:
time: 436 us
  Pallas kernels  420 us (96%)
  local copies, waits for them, and re-layouts  13.9 us (3%)
    pallas_call x1, Pallas kernels, body(): pl.pallas_call(lanczos, out_shape=(pltpu.VMEM((STEPS + 1, 2, ROWS, LANES)...  411 us
    mul x4, local copies, waits for them, and re-layouts, body(): site_loc[:, :, None, :, None] * eye[None, None, :, None, :]  13.3 us
    pallas_call x1, Pallas kernels, body(): pl.pallas_call(write_out, out_shape=jax.ShapeDtypeStruct((STEPS + 1, D, 4...  9.61 us

profile of v1, /device:TPU:1, one launch (start us, length us, event | category | flops | bytes accessed | tf_op | source)
XLA Modules:
  0.0 435.8 jit_solution(6308925536876637396)
XLA Ops:
  0.6 4.3 mul.20
  4.9 7.8 %mul.21 = bf16[6,256,256]{2,1,0:T(8,128)(2,1)S(1)} reshape(bf16[6,16,16,16,16]{4,3,2,1,0:T(8,128)(2,1)} %mul.20) | data formatting | bytes 1572864 | tf_op jit(solution)/shard_map/mul | solution.py:354
  12.7 0.2 mul.22
  13.0 1.0 mul.23
  13.9 0.9 broadcast_multiply_fusion.kron_hbm
  14.9 410.7 %lanczos.1 = (f32[7,2,4096,128]{3,2,1,0:T(8,128)S(1)}, f32[2,6,8,128]{3,2,1,0:T(8,128)S(1)}) custom-call(f32[256,4,4,256]{3,2,1,0:T(4,128)} %psi_hbm.1, bf16[6,256,256]{2,1,0:T(8,128)(2,1)} %left_hbm.1, bf16[6,256,256]{2,1,0:T(8,128)(2,1)} %broadcast_multiply_fusion.kron_hbm, bf16[6,256,256]{2,1,0:T(8,128)(2,1)} %right_hbm.1), custom_call_target="tpu_custom_call" | custom-call | tf_op jit(solution)/shard_map/lanczos/pallas_call | solution.py:355
  425.6 0.6 slice_reduce_fusion
  426.2 9.6 %write_out.1 = f32[7,256,4,4,256]{4,3,2,1,0:T(4,128)} custom-call(f32[7,2,4096,128]{3,2,1,0:T(8,128)S(1)} %get-tuple-element.5.kry), custom_call_target="tpu_custom_call" | custom-call | tf_op jit(solution)/shard_map/write_out/pallas_call | solution.py:385
  (1 shorter events, 0.0 us)

commit v2 on v1

v2 whole, which is shorter than its diff:
```python
import jax
import jax.numpy as jnp
from jax import lax
from jax.experimental import pallas as pl
from jax.experimental.pallas import tpu as pltpu
from jax.sharding import PartitionSpec as P

STEPS = 6
D = 256
PAIR = 16
ROWS = PAIR * D
LANES = 128
TERMS = 6
XN, YN, ZN = 4, 4, 8
F32 = jnp.float32
BF16 = jnp.bfloat16
MESH_ID = pl.DeviceIdType.MESH

S1, S2, S3, S4, S5, S6 = range(6)
T1, T2, T3, T4, T5, T6 = range(6, 12)
ZR = 12
ZG = 19
G1, G2, G3, G4 = range(26, 30)
H0 = 30
NSEM = 46
CROSS = 7
GROUPS = 4


def rows(start, size):
    return pl.ds(pl.multiple_of(start, 8), size)


def lanczos(psi_hbm, left_hbm, site_hbm, right_hbm, kry, ab, u, y1, y2, part, lbuf, rbuf, wraw, wbuf, relay1, final1, relay2, final2, zrecv, load_sem, send_sem, recv_sem, c_send, c_recv, x_send, x_recv):
    me = lax.axis_index("terms")
    core = me % 2
    x = (me // 2) % XN
    y = (me // 8) % YN
    z = me // 32

    def dev(xx, yy, zz, cc):
        return (((zz * YN + yy) * XN + xx) * 2 + cc,)

    xr, xl = dev((x + 1) % XN, y, z, core), dev((x + 3) % XN, y, z, core)
    yr, yl = dev(x, (y + 1) % YN, z, core), dev(x, (y + 3) % YN, z, core)
    zdev = [None] + [dev(x, y, (z + d) % ZN, core) for d in range(1, ZN)]
    other = dev(x, y, z, 1 - core)

    barrier = pltpu.get_barrier_semaphore()
    peers = [xr, xl, yr, yl, other] + zdev[1:]
    for peer in peers:
        pl.semaphore_signal(barrier, inc=1, device_id=peer, device_id_type=MESH_ID)

    loads = []
    for h in range(2):
        for s in range(4):
            for t in range(4):
                loads.append(pltpu.make_async_copy(psi_hbm.at[:, s, t, pl.ds(h * LANES, LANES)], kry.at[0, h, pl.ds((s * 4 + t) * D, D)], load_sem.at[0]))
    for cp in loads:
        cp.start()
    mine = pl.multiple_of(core * TERMS, TERMS)
    own = []
    for k in range(TERMS):
        own.append(pltpu.make_async_copy(left_hbm.at[k], lbuf.at[:, pl.ds(pl.multiple_of((mine + k) * D, D), D)], load_sem.at[1]))
        own.append(pltpu.make_async_copy(right_hbm.at[k, :, pl.ds(pl.multiple_of(core * LANES, LANES), LANES)], rbuf.at[mine + k], load_sem.at[1]))
    own.append(pltpu.make_async_copy(site_hbm, wraw.at[pl.ds(mine, TERMS)], load_sem.at[1]))
    for cp in own:
        cp.start()

    pl.semaphore_wait(barrier, len(peers))

    swaps = []

    def swap(src, dst, i):
        swaps.append(pltpu.make_async_remote_copy(src, dst, x_send.at[i], x_recv.at[i], device_id=other, device_id_type=MESH_ID))

    swap(site_hbm, wraw.at[pl.ds(mine, TERMS)], 2 * TERMS)
    for k in range(TERMS):
        swap(left_hbm.at[k], lbuf.at[:, pl.ds(pl.multiple_of((mine + k) * D, D), D)], 2 * k)
        swap(right_hbm.at[k, :, pl.ds(pl.multiple_of((1 - core) * LANES, LANES), LANES)], rbuf.at[mine + k], 2 * k + 1)
    for cp in swaps:
        cp.start()

    CH = 256
    NCH = ROWS // CH

    for cp in loads:
        cp.wait()

    def chunk(i):
        return i // NCH, rows((i % NCH) * CH, CH)

    def fold(val):
        return jnp.sum(val.reshape(CH // 64, 64, LANES), axis=0)

    zero = jnp.zeros((64, LANES), F32)

    def total(acc):
        return jnp.broadcast_to(jnp.sum(acc, keepdims=True), (8, LANES))

    def wide(val):
        return jnp.broadcast_to(val[:1], (CH, LANES))

    def sumsq(i, acc):
        h, r = chunk(i)
        val = kry[0, h, r, :]
        return acc + fold(val * val)

    norm0 = jnp.sqrt(total(lax.fori_loop(0, 2 * NCH, sumsq, zero)))
    inv0 = wide(1.0 / norm0)

    def scale0(i, carry):
        h, r = chunk(i)
        val = kry[0, h, r, :] * inv0
        kry[0, h, r, :] = val
        u[h, r, :] = val.astype(BF16)
        return carry

    lax.fori_loop(0, 2 * NCH, scale0, 0)
    for cp in own:
        cp.wait()
    for cp in swaps:
        cp.wait()

    spread_rows = (lax.broadcasted_iota(jnp.int32, (D, PAIR), 0) // 16 == lax.broadcasted_iota(jnp.int32, (D, PAIR), 1)).astype(BF16)
    spread_cols = (lax.broadcasted_iota(jnp.int32, (PAIR, D), 1) // 16 == lax.broadcasted_iota(jnp.int32, (PAIR, D), 0)).astype(BF16)
    same = lax.broadcasted_iota(jnp.int32, (D, D), 0) % 16 == lax.broadcasted_iota(jnp.int32, (D, D), 1) % 16

    def build(k, carry):
        tall = jnp.dot(spread_rows, wraw[k], preferred_element_type=F32).astype(BF16)
        full = jnp.dot(tall, spread_cols, preferred_element_type=F32)
        wbuf[k] = jnp.where(same, full, 0.0).astype(BF16)
        return carry

    lax.fori_loop(0, 2 * TERMS, build, 0)

    def right_product(g):
        weights = jnp.concatenate([rbuf[2 * g], rbuf[2 * g + 1]], axis=1)
        for m in range(4):
            r = pl.ds(m * 1024, 1024)
            lhs = jnp.concatenate([u[0, r, :], u[1, r, :]], axis=1)
            res = jnp.dot(lhs, weights, preferred_element_type=F32).astype(BF16)
            y1[2 * g, r, :] = res[:, :LANES]
            y1[2 * g + 1, r, :] = res[:, LANES:]

    def site_product(g, half):
        for t in range(2):
            k = 2 * g + t
            w = wbuf[k, pl.ds(128 * half, 128), :]
            for m in range(8):
                cols = []
                for b in range(2):
                    cols.append(jnp.concatenate([y1[k, pl.ds(p * D + 32 * m + 16 * b, 16), :] for p in range(PAIR)], axis=0))
                res = jnp.dot(w, jnp.concatenate(cols, axis=1), preferred_element_type=F32).astype(BF16)
                for b in range(2):
                    for q in range(8):
                        y2[q, rows(k * D + 32 * m + 16 * b, 16), :] = res[16 * q : 16 * q + 16, b * LANES : (b + 1) * LANES]

    def left_product(half, qs):
        rhs = jnp.concatenate([y2[q] for q in qs], axis=1)
        res = jnp.dot(lbuf[...], rhs, preferred_element_type=F32)
        for i, q in enumerate(qs):
            part[rows((8 * half + q) * D, D), :] = res[:, i * LANES : (i + 1) * LANES]

    ring1 = [(x, xr, xl), (y, yr, yl)] * 2
    ring2 = [(y, yr, yl), (x, xr, xl)] * 2
    ALL = range(GROUPS)
    HALVES = [(0, 1), (2, 3)]

    def chunk_at(n, d):
        return 4 * n * D + D * ((ring1[n][0] + d) % 4)

    def block_at(n, d1, d2):
        return chunk_at(n, d1) + 64 * ((ring2[n][0] + d2) % 4)

    def step(j, beta_prev):
        nxt = j + 1
        turn = j % 2
        sends = []

        def start(src, dst, n, s, device):
            cp = pltpu.make_async_remote_copy(src, dst, send_sem.at[n, s], recv_sem.at[n, s], device_id=device, device_id_type=MESH_ID)
            cp.start()
            sends.append(cp)
            return cp

        def add_into(first, size, refs):
            for o in range(0, size, 128):
                m = min(128, size - o)
                acc = part[rows(first + o, m), :]
                for ref in refs:
                    acc = acc + ref[pl.ds(o, m), :]
                part[rows(first + o, m), :] = acc

        one = [[None] * 6 for _ in ALL]
        two = [[None] * 6 for _ in ALL]

        def scatter1_first(n, d):
            _, right, left = ring1[n]
            first = chunk_at(n, d)
            if d == 2:
                one[n][0] = start(part.at[rows(first, 128)], relay1.at[n, 0], n, S1, right)
                one[n][1] = start(part.at[rows(first + 128, 128)], relay1.at[n, 1], n, S2, left)
            elif d == 1:
                one[n][2] = start(part.at[rows(first + 128, 128)], final1.at[n, 0, pl.ds(128, 128)], n, S3, right)
            elif d == 3:
                one[n][3] = start(part.at[rows(first, 128)], final1.at[n, 1, pl.ds(0, 128)], n, S4, left)

        def scatter1_relay(n):
            _, right, left = ring1[n]
            one[n][0].wait_recv()
            add_into(chunk_at(n, 1), 128, [relay1.at[n, 0]])
            one[n][4] = start(part.at[rows(chunk_at(n, 1), 128)], final1.at[n, 0, pl.ds(0, 128)], n, S5, right)
            one[n][1].wait_recv()
            add_into(chunk_at(n, 3) + 128, 128, [relay1.at[n, 1]])
            one[n][5] = start(part.at[rows(chunk_at(n, 3) + 128, 128)], final1.at[n, 1, pl.ds(128, 128)], n, S6, left)

        def scatter1_final(n):
            for i in (2, 3, 4, 5):
                one[n][i].wait_recv()
            add_into(chunk_at(n, 0), 256, [final1.at[n, 0], final1.at[n, 1]])
            _, right, left = ring2[n]
            two[n][0] = start(part.at[rows(block_at(n, 0, 2), 32)], relay2.at[n, 0], n, T1, right)
            two[n][1] = start(part.at[rows(block_at(n, 0, 2) + 32, 32)], relay2.at[n, 1], n, T2, left)
            two[n][2] = start(part.at[rows(block_at(n, 0, 1) + 32, 32)], final2.at[n, 0, pl.ds(32, 32)], n, T3, right)
            two[n][3] = start(part.at[rows(block_at(n, 0, 3), 32)], final2.at[n, 1, pl.ds(0, 32)], n, T4, left)

        def scatter2_relay(n):
            _, right, left = ring2[n]
            two[n][0].wait_recv()
            add_into(block_at(n, 0, 1), 32, [relay2.at[n, 0]])
            two[n][4] = start(part.at[rows(block_at(n, 0, 1), 32)], final2.at[n, 0, pl.ds(0, 32)], n, T5, right)
            two[n][1].wait_recv()
            add_into(block_at(n, 0, 3) + 32, 32, [relay2.at[n, 1]])
            two[n][5] = start(part.at[rows(block_at(n, 0, 3) + 32, 32)], final2.at[n, 1, pl.ds(32, 32)], n, T6, left)

        far_first = (4, 3, 5, 2, 6, 1, 7)
        zr = [[None] * ZN for _ in ALL]
        zg = [[None] * ZN for _ in ALL]

        def scatter2_final(n):
            for i in (2, 3, 4, 5):
                two[n][i].wait_recv()
            add_into(block_at(n, 0, 0), 64, [final2.at[n, 0], final2.at[n, 1]])

        def scatter_z(group):
            for d in far_first:
                for n in group:
                    zr[n][d] = start(part.at[rows(block_at(n, 0, 0) + 8 * ((z + d) % ZN), 8)], zrecv.at[n, d], n, ZR + d - 1, zdev[d])

        def finish_z(group):
            for n in group:
                r = rows(block_at(n, 0, 0) + 8 * z, 8)
                acc = part[r, :]
                for d in range(1, ZN):
                    zr[n][d].wait_recv()
                    acc = acc + zrecv[n, d]
                kry[nxt, core, r, :] = acc
            for d in far_first:
                for n in group:
                    r = rows(block_at(n, 0, 0) + 8 * z, 8)
                    zg[n][d] = start(kry.at[nxt, core, r], kry.at[nxt, core, r], n, ZG + d - 1, zdev[d])

        def spread(n, first, size, s, device):
            r = rows(first, size)
            return start(kry.at[nxt, core, r], kry.at[nxt, core, r], n, s, device)

        g2 = [[None] * 4 for _ in ALL]
        g1 = [[[None] * 4 for _ in range(4)] for _ in ALL]
        crossing = [[] for _ in ALL]

        def cross(n, first, size):
            r = rows(first, size)
            i = len(crossing[n])
            cp = pltpu.make_async_remote_copy(kry.at[nxt, core, r], kry.at[nxt, core, r], c_send.at[turn, n, i], c_recv.at[turn, n, i], device_id=other, device_id_type=MESH_ID)
            cp.start()
            sends.append(cp)
            crossing[n].append(cp)

        def block_out(n, d2):
            _, right, left = ring1[n]
            g1[n][d2][0] = spread(n, block_at(n, 0, d2), 64, H0 + 4 * d2, right)
            g1[n][d2][1] = spread(n, block_at(n, 0, d2), 64, H0 + 4 * d2 + 1, left)

        def block_on(n, d2):
            _, right, left = ring1[n]
            g1[n][d2][0].wait_recv()
            g1[n][d2][2] = spread(n, block_at(n, 3, d2), 32, H0 + 4 * d2 + 2, right)
            g1[n][d2][1].wait_recv()
            g1[n][d2][3] = spread(n, block_at(n, 1, d2) + 32, 32, H0 + 4 * d2 + 3, left)

        def gather2_first(n):
            for d in range(1, ZN):
                zg[n][d].wait_recv()
            _, right, left = ring2[n]
            g2[n][0] = spread(n, block_at(n, 0, 0), 64, G1, right)
            g2[n][1] = spread(n, block_at(n, 0, 0), 64, G2, left)
            block_out(n, 0)

        def gather2_relay(n):
            _, right, left = ring2[n]
            g2[n][0].wait_recv()
            g2[n][2] = spread(n, block_at(n, 0, 3), 32, G3, right)
            g2[n][1].wait_recv()
            g2[n][3] = spread(n, block_at(n, 0, 1) + 32, 32, G4, left)
            block_out(n, 3)
            block_out(n, 1)

        def gather2_far(n):
            g2[n][2].wait_recv()
            g2[n][3].wait_recv()
            block_out(n, 2)
            cross(n, chunk_at(n, 0), 256)

        def gather1_last(n):
            for d2 in (0, 3, 1, 2):
                g1[n][d2][2].wait_recv()
                g1[n][d2][3].wait_recv()
                cross(n, block_at(n, 2, d2), 64)

        right_product(0)

        def pair_step(g, carry):
            site_product(g, 0)
            right_product(g + 1)
            return carry

        lax.fori_loop(0, TERMS - 1, pair_step, 0)
        site_product(TERMS - 1, 0)

        def site_second(i, carry):
            site_product(2 * i, 1)
            site_product(2 * i + 1, 1)
            return carry

        for half in range(2):
            if half == 1:
                lax.fori_loop(0, TERMS // 2, site_second, 0)
            for ds in ((2, 1), (3, 0)):
                left_product(half, [(x + d) % 4 for d in ds] + [4 + (y + d) % 4 for d in ds])
                for d in ds:
                    for n in HALVES[half]:
                        scatter1_first(n, d)

        def both(*stages):
            for group in HALVES:
                for stage in stages:
                    for n in group:
                        stage(n)

        both(scatter1_relay)
        both(scatter1_final)
        both(scatter2_relay)
        for group in HALVES:
            for n in group:
                scatter2_final(n)
            scatter_z(group)
        for group in HALVES:
            finish_z(group)
        both(gather2_first)
        both(gather2_relay)
        both(gather2_far, lambda n: block_on(n, 0))
        both(lambda n: block_on(n, 3), lambda n: block_on(n, 1))

        def neighbours_done(n):
            block_on(n, 2)
            cross(n, chunk_at(n, 3), 256)
            cross(n, chunk_at(n, 1), 256)

        both(neighbours_done)
        both(gather1_last)

        prev = jnp.maximum(j - 1, 0)
        acc = zero
        for half in range(2):
            for n in HALVES[half]:
                for cp in crossing[n]:
                    cp.wait_recv()

            def dot_chunk(i, total_so_far):
                hh = i // (NCH // 2)
                r = rows(half * (ROWS // 2) + (i % (NCH // 2)) * CH, CH)
                return total_so_far + fold(kry[nxt, hh, r, :] * kry[j, hh, r, :])

            acc = lax.fori_loop(0, NCH, dot_chunk, acc)
        alpha = total(acc)
        al = wide(alpha)
        bp = wide(beta_prev)

        def resid_chunk(i, total_so_far):
            hh, r = chunk(i)
            val = kry[nxt, hh, r, :] - al * kry[j, hh, r, :] - bp * kry[prev, hh, r, :]
            kry[nxt, hh, r, :] = val
            return total_so_far + fold(val * val)

        for cp in sends:
            cp.wait_send()
        beta = jnp.sqrt(total(lax.fori_loop(0, 2 * NCH, resid_chunk, zero)))
        inv = wide(1.0 / beta)

        def scale_chunk(i, carry):
            hh, r = chunk(i)
            val = kry[nxt, hh, r, :] * inv
            kry[nxt, hh, r, :] = val
            u[hh, r, :] = val.astype(BF16)
            return carry

        lax.fori_loop(0, 2 * NCH, scale_chunk, 0)
        ab[0, j] = alpha
        ab[1, j] = beta
        return beta

    lax.fori_loop(0, STEPS, step, jnp.zeros((8, LANES), F32))


def write_out(kry, out, sem):
    copies = []
    for h in range(2):
        for s in range(4):
            for t in range(4):
                copies.append(pltpu.make_async_copy(kry.at[:, h, pl.ds((s * 4 + t) * D, D)], out.at[:, :, s, t, pl.ds(h * LANES, LANES)], sem))
    for cp in copies:
        cp.start()
    for cp in copies:
        cp.wait()


def solution(mesh):
    anywhere = pl.BlockSpec(memory_space=pl.ANY)
    vmem = pl.BlockSpec(memory_space=pltpu.VMEM)

    def body(psi, left_loc, site_loc, right_loc):
        kry, ab = pl.pallas_call(
            lanczos,
            out_shape=(pltpu.VMEM((STEPS + 1, 2, ROWS, LANES), F32), pltpu.VMEM((2, STEPS, 8, LANES), F32)),
            in_specs=[anywhere] * 4,
            out_specs=(vmem, vmem),
            scratch_shapes=[
                pltpu.VMEM((2, ROWS, LANES), BF16),
                pltpu.VMEM((2 * TERMS, ROWS, LANES), BF16),
                pltpu.VMEM((PAIR // 2, 2 * TERMS * D, LANES), BF16),
                pltpu.VMEM((ROWS, LANES), F32),
                pltpu.VMEM((D, 2 * TERMS * D), BF16),
                pltpu.VMEM((2 * TERMS, D, LANES), BF16),
                pltpu.VMEM((2 * TERMS, PAIR, PAIR), BF16),
                pltpu.VMEM((2 * TERMS, D, D), BF16),
                pltpu.VMEM((GROUPS, 2, 128, LANES), F32),
                pltpu.VMEM((GROUPS, 2, 256, LANES), F32),
                pltpu.VMEM((GROUPS, 2, 32, LANES), F32),
                pltpu.VMEM((GROUPS, 2, 64, LANES), F32),
                pltpu.VMEM((GROUPS, ZN, 8, LANES), F32),
                pltpu.SemaphoreType.DMA((2,)),
                pltpu.SemaphoreType.DMA((GROUPS, NSEM)),
                pltpu.SemaphoreType.DMA((GROUPS, NSEM)),
                pltpu.SemaphoreType.DMA((2, GROUPS, CROSS)),
                pltpu.SemaphoreType.DMA((2, GROUPS, CROSS)),
                pltpu.SemaphoreType.DMA((2 * TERMS + 1,)),
                pltpu.SemaphoreType.DMA((2 * TERMS + 1,)),
            ],
            compiler_params=pltpu.CompilerParams(collective_id=0, has_side_effects=True, vmem_limit_bytes=32 * 2**20),
            name="lanczos",
        )(*(pltpu.with_memory_space_constraint(arr, pltpu.HBM) for arr in (psi, left_loc, site_loc, right_loc)))
        krylov = pl.pallas_call(
            write_out,
            out_shape=jax.ShapeDtypeStruct((STEPS + 1, D, 4, 4, D), F32),
            in_specs=[vmem],
            out_specs=anywhere,
            scratch_shapes=[pltpu.SemaphoreType.DMA],
            compiler_params=pltpu.CompilerParams(vmem_limit_bytes=2**20),
            name="write_out",
        )(pltpu.with_memory_space_constraint(kry, pltpu.VMEM))
        return krylov, ab[0, :, 0, 0], ab[1, :, 0, 0]

    return jax.shard_map(body, mesh=mesh, in_specs=(P(), P("terms"), P("terms"), P("terms")), out_specs=(P(), P(), P()), check_vma=False)
```

time: 436 us -> 368 us (0.84)
  Pallas kernels: 420 us -> 367 us
  local copies, waits for them, and re-layouts: 13.9 us -> 0.64 us
    pallas_call x1, Pallas kernels: 411 us -> 357 us  [body(): pl.pallas_call(lanczos, out_shape=(pltpu.VMEM((STEPS + 1, 2, ROWS, LANES)...]
    mul x4 -> x0, local copies, waits for them, and re-layouts: 13.3 us -> none  [body(): site_loc[:, :, None, :, None] * eye[None, None, :, None, :]]
where the time goes in v2:
time: 368 us
  Pallas kernels  367 us (100%)
    pallas_call x1, Pallas kernels, body(): pl.pallas_call(lanczos, out_shape=(pltpu.VMEM((STEPS + 1, 2, ROWS, LANES)...  357 us
    pallas_call x1, Pallas kernels, body(): pl.pallas_call(write_out, out_shape=jax.ShapeDtypeStruct((STEPS + 1, D, 4...  9.61 us

profile of v2, /device:TPU:1, one launch (start us, length us, event | category | flops | bytes accessed | tf_op | source)
XLA Modules:
  0.0 367.8 jit_solution(14730519610858666870)
XLA Ops:
  0.6 356.9 %lanczos.1 = (f32[7,2,4096,128]{3,2,1,0:T(8,128)S(1)}, f32[2,6,8,128]{3,2,1,0:T(8,128)S(1)}) custom-call(f32[256,4,4,256]{3,2,1,0:T(4,128)} %psi_hbm.1, bf16[6,256,256]{2,1,0:T(8,128)(2,1)} %left_hbm.1, bf16[6,16,16]{2,1,0:T(8,128)(2,1)} %site_hbm.1, bf16[6,256,256]{2,1,0:T(8,128)(2,1)} %right_hbm.1), custom_call_target="tpu_custom_call" | custom-call | tf_op jit(solution)/shard_map/lanczos/pallas_call | solution.py:433
  357.6 0.6 slice_reduce_fusion
  358.2 9.6 %write_out.1 = f32[7,256,4,4,256]{4,3,2,1,0:T(4,128)} custom-call(f32[7,2,4096,128]{3,2,1,0:T(8,128)S(1)} %get-tuple-element.5.kry), custom_call_target="tpu_custom_call" | custom-call | tf_op jit(solution)/shard_map/write_out/pallas_call | solution.py:463
